TPU v7x, 32 devices: a whole 2x2x4 slice. The times are simulated.
32 devices in a mesh: ens: 2 (over y), gx: 16 (over z, x, core).
Axes of the slice: x: 2, y: 2, z: 4, core: 2. Of those that a mesh axis runs over, the one named last changes fastest.
Arguments:
- model_state: float32 [8, 4, 320, 2560], P('ens', None, 'gx'), parts along dimension 0, may hold values from -6 to 6
- driving: float32 [8, 4, 320, 2560], P('ens', None, 'gx'), parts along dimension 0, may hold values from -12 to 12
- mode_east: int32 [30], replicated, may hold values from 1 to 60, as said below
- mode_north: int32 [30], replicated, may hold values from 1 to 60, as said below
- level_class: int32 [4], replicated, may hold values from 0 to 7
- nudge_table: float32 [8, 4], replicated, may hold values from 0.05 to 0.5
Outputs:
- nudged: float32 [8, 4, 320, 2560], P('ens', None, 'gx'), parts along dimension 0
- residual_log: float32 [8, 4], P('ens'), parts along dimension 0
There are 2 independent parts, one for each index of `ens`. A program takes and returns all parts, laid end to end along the dimension named above; an argument that names none is the same for every part. Nothing has to cross between parts.
Inputs may be any that keep to these rules, and one draw needn't show every extreme that they name: `mode_east`: 30 distinct wavenumbers in increasing order, the first 1 and the last 60. `mode_north`: 30 distinct wavenumbers in increasing order, the first 1 and the last 60.
All inputs are finite; a program needn't handle non-finite values.
Results may differ from a plain program's by a relative error of at most 0.0001.
Values sent between devices are 32-bit elements; how exact they have to be, the bound alone decides.
A program may use at most 128 MiB of HBM per device.

v0:
```python
import jax
import jax.numpy as jnp
from jax import lax
from jax.sharding import PartitionSpec as P

ITERS = 4


DIFFUSION = 0.24


def extended_2(cells, sides, width):
    for axis, dim in sides:
        count = lax.axis_size(axis)
        ends = count - 1
        head = lax.slice_in_dim(cells, 0, width, axis=dim)
        tail = lax.slice_in_dim(cells, cells.shape[dim] - width, cells.shape[dim], axis=dim)
        cells = jnp.concatenate(
            [
                lax.ppermute(tail, axis, [(i, (i + 1) % count) for i in range(ends)]),
                cells,
                lax.ppermute(head, axis, [((i + 1) % count, i) for i in range(ends)]),
            ],
            axis=dim,
        )
    return cells


def sine_table(wavenums, first_cell, span_cols, grid_cells):
    places = first_cell + lax.iota(jnp.int32, span_cols) + 1
    phases = wavenums[:, None] * places[None, :] % (2 * (grid_cells + 1))
    return jnp.sin(phases.astype(jnp.float32) * (jnp.pi / (grid_cells + 1)))


def laplace(extended):
    centre = extended[:, :, 1:-1]
    padded = jnp.pad(centre, ((0, 0), (0, 0), (0, 0), (1, 1)))
    return (
        extended[:, :, 2:]
        + extended[:, :, :-2]
        + padded[:, :, :, 2:]
        + padded[:, :, :, :-2]
        - 4.0 * centre
    )


def local(model_state, driving, mode_east, mode_north, level_class, nudge_table):
    fields, levels, columns, north_cells = model_state.shape
    tiles = lax.axis_size("gx")
    first_col = lax.axis_index("gx") * columns
    total_east = columns * tiles
    scale_norm = 4.0 / ((total_east + 1) * (north_cells + 1))
    cell_count = float(levels * total_east * north_cells)
    table_north = sine_table(mode_north, 0, north_cells, north_cells)
    table_own = sine_table(mode_east, first_col, columns, total_east)
    one_hot = (level_class[:, None] == lax.iota(jnp.int32, nudge_table.shape[0])[None, :]).astype(
        jnp.float32
    )
    weights = jnp.dot(one_hot, nudge_table, precision=lax.Precision.HIGHEST).T[:, :, None, None]
    records = []
    extended = extended_2(model_state, (("gx", 2),), ITERS)
    for substep in range(ITERS):
        reach_now = ITERS - substep
        current = extended[:, :, reach_now : reach_now + columns]
        along_north = jnp.dot(
            (driving - current).reshape(-1, north_cells),
            table_north.T,
            precision=lax.Precision.HIGHEST,
        )
        along_north = along_north.reshape(fields, levels, columns, -1)
        mode_partial_value = (
            jnp.einsum("flxb,ax->flab", along_north, table_own, precision=lax.Precision.HIGHEST)
            * scale_norm
        )
        coeffs = lax.psum(mode_partial_value, "gx")
        lead_col = first_col - (reach_now - 1)
        span_cols = columns + 2 * (reach_now - 1)
        table_wide = sine_table(mode_east, lead_col, span_cols, total_east)
        global_col = lead_col + lax.iota(jnp.int32, span_cols)
        inside = ((global_col >= 0) & (global_col < total_east))[None, None, :, None]
        partial_value = jnp.einsum(
            "flab,ax->flxb", coeffs, table_wide, precision=lax.Precision.HIGHEST
        )
        rebuild_span_cols = table_wide.shape[1]
        flat = jnp.dot(
            partial_value.reshape(-1, partial_value.shape[-1]),
            table_north,
            precision=lax.Precision.HIGHEST,
        )
        updated = (
            extended[:, :, 1:-1]
            + flat.reshape(fields, levels, rebuild_span_cols, north_cells) * weights
            + DIFFUSION * laplace(extended)
        )
        extended = jnp.where(inside, updated, 0.0)
        current = extended[:, :, reach_now - 1 : reach_now - 1 + columns]
        remain = driving - current
        squares = jnp.sum(remain * remain, axis=(1, 2, 3))
        records.append(lax.psum(squares, "gx"))
    stacked = jnp.stack(records)
    return (current, jnp.sqrt(stacked / cell_count))


def solution(mesh):
    return jax.shard_map(
        local,
        mesh=mesh,
        in_specs=(P("ens", None, "gx", None), P("ens", None, "gx", None), P(), P(), P(), P()),
        out_specs=(P("ens", None, "gx", None), P("ens", None)),
        check_vma=False,
    )
```

profile of v0, /device:TPU:0, one launch (start us, length us, event | category | flops | bytes accessed | tf_op | source)
XLA Modules:
  0.0 384.8 jit_solution(12978652984436395358)
XLA Ops:
  0.7 3.1 copy.8
  3.8 1.9 copy-done.2
  5.7 1.2 fusion.219
  6.9 3.3 collective-permute-start
  10.2 1.3 collective-permute-start.1
  13.4 3.6 sub.42
  17.0 4.7 %fusion.29 = f32[4,4,20,30]{3,2,1,0:T(8,128)S(1)} fusion(f32[4,4,20,2560]{3,1,2,0:T(4,128)S(1)} %sub.42, s32[2560]{0:T(1024)S(1)} %iota_add_fusion, s32[30]{0:T(128)S(1)} %copy-done.7), kind=kOutput, calls=%fused_computation.49 | convolution fusion | flops 295603200 | bytes 3325560 | tf_op jit(solution)/shard_map/dot_general | solution.py:65
  23.1 67.1 %psum.56 = f32[4,4,30,30]{3,1,0,2:T(4,128)S(1)} all-reduce(f32[4,4,30,30]{3,1,0,2:T(4,128)} %bitcast.73), channel_id=1, replica_groups=mesh['ens'=2,'gx'=16] {'gx'}, use_global_device_ids=true, to_apply=%region_0.1 | all-reduce | flops 14400 | bytes 115200 | tf_op jit(solution)/shard_map/psum | solution.py:75
  91.9 3.2 pad_maximum_fusion
  96.0 6.8 %fusion.5 = f32[4,4,26,2560]{3,2,1,0:T(8,128)S(1)} fusion(f32[4,4,26,2560]{3,2,1,0:T(8,128)S(1)} %slice.106, f32[4,4,28,2560]{3,2,1,0:T(8,128)S(1)} %pad_maximum_fusion, f32[4,4,26,30]{3,2,1,0:T(8,128)S(1)} %convolution_bitcast_fusion, f32[4,4]{1,0:T(4,128)S(1)} %copy.11, pred[26]{0:T(512)(128)(4,1)S(1)} %compare_and_fusion, s32[2560]{0:T(1024)S(1)} %iota_add_fusion, ...), kind=kOutput, calls=%fused_computation.7 | convolution fusion | flops 394726400 | bytes 17099730 | tf_op jit(solution)/shard_map/dot_general | solution.py:85
  102.9 5.4 %fusion.32 = f32[4,4,20,30]{3,2,1,0:T(8,128)S(1)} fusion(f32[4,4,20,2560]{3,1,2,0:T(4,128)S(1)} %copy-done.1, f32[4,4,26,2560]{3,2,1,0:T(8,128)S(1)} %fusion.5, s32[2560]{0:T(1024)S(1)} %iota_add_fusion, s32[30]{0:T(128)S(1)} %copy-done.7), kind=kOutput, calls=%fused_computation.55 | convolution fusion | flops 296422400 | bytes 7260160 | tf_op jit(solution)/shard_map/dot_general | solution.py:65
  108.3 2.5 slice.109
  112.2 60.4 %psum.57 = f32[4,4,30,30]{3,1,0,2:T(4,128)S(1)} all-reduce(f32[4,4,30,30]{3,1,0,2:T(4,128)} %bitcast.74), channel_id=1, replica_groups=mesh['ens'=2,'gx'=16] {'gx'}, use_global_device_ids=true, to_apply=%region_1.2 | all-reduce | flops 14400 | bytes 115200 | tf_op jit(solution)/shard_map/psum | solution.py:75
  173.7 10.2 %fusion.12 = f32[4,4,24,2560]{3,2,1,0:T(8,128)S(1)} fusion(f32[4,4,24,2560]{3,2,1,0:T(8,128)} %slice.109, f32[4,4,24,30]{3,2,1,0:T(8,128)S(1)} %convolution_bitcast_fusion.3, f32[4,4,26,2560]{3,2,1,0:T(8,128)} %copy-done.5, f32[4,4]{1,0:T(4,128)S(1)} %copy.11, pred[24]{0:T(512)(128)(4,1)} %compare_and_fusion.1, s32[2560]{0:T(1024)S(1)} %iota_add_fusion, ...), kind=kOutput, calls=%fused_computation.19 | convolution fusion | flops 364416000 | bytes 15785168 | tf_op jit(solution)/shard_map/dot_general | solution.py:85
  184.0 5.2 %fusion.33 = f32[4,4,20,30]{3,2,1,0:T(8,128)S(1)} fusion(f32[4,4,20,2560]{3,1,2,0:T(4,128)S(1)} %copy-done.1, f32[4,4,24,2560]{3,2,1,0:T(8,128)S(1)} %fusion.12, s32[2560]{0:T(1024)S(1)} %iota_add_fusion, s32[30]{0:T(128)S(1)} %copy-done.7), kind=kOutput, calls=%fused_computation.56 | convolution fusion | flops 296422400 | bytes 7257720 | tf_op jit(solution)/shard_map/dot_general | solution.py:65
  189.2 2.5 slice.113
  193.0 60.6 %psum.58 = f32[4,4,30,30]{3,1,0,2:T(4,128)S(1)} all-reduce(f32[4,4,30,30]{3,1,0,2:T(4,128)} %bitcast.75), channel_id=1, replica_groups=mesh['ens'=2,'gx'=16] {'gx'}, use_global_device_ids=true, to_apply=%region_2.3 | all-reduce | flops 14400 | bytes 115200 | tf_op jit(solution)/shard_map/psum | solution.py:75
  254.7 9.9 %fusion.13 = f32[4,4,22,2560]{3,2,1,0:T(8,128)S(1)} fusion(f32[4,4,22,2560]{3,2,1,0:T(8,128)} %slice.113, f32[4,4,22,30]{3,2,1,0:T(8,128)S(1)} %convolution_bitcast_fusion.2, f32[4,4,24,2560]{3,2,1,0:T(8,128)} %copy-done.3, f32[4,4]{1,0:T(4,128)S(1)} %copy.11, pred[22]{0:T(512)(128)(4,1)} %compare_and_fusion.2, s32[2560]{0:T(1024)S(1)} %iota_add_fusion, ...), kind=kOutput, calls=%fused_computation.20 | convolution fusion | flops 334105600 | bytes 14470606 | tf_op jit(solution)/shard_map/dot_general | solution.py:85
  264.7 5.2 %fusion.31 = f32[4,4,20,30]{3,2,1,0:T(8,128)S(1)} fusion(f32[4,4,20,2560]{3,1,2,0:T(4,128)S(1)} %copy-done.1, s32[2560]{0:T(1024)S(1)} %iota_add_fusion, s32[30]{0:T(128)S(1)} %copy-done.7, f32[4,4,22,2560]{3,2,1,0:T(8,128)S(1)} %fusion.13), kind=kOutput, calls=%fused_computation.54 | convolution fusion | flops 296422400 | bytes 6930040 | tf_op jit(solution)/shard_map/dot_general | solution.py:65
  269.9 2.4 slice.117
  273.6 60.6 %psum.59 = f32[4,4,30,30]{3,1,0,2:T(4,128)S(1)} all-reduce(f32[4,4,30,30]{3,1,0,2:T(4,128)} %bitcast.76), channel_id=1, replica_groups=mesh['ens'=2,'gx'=16] {'gx'}, use_global_device_ids=true, to_apply=%region_3.4 | all-reduce | flops 14400 | bytes 115200 | tf_op jit(solution)/shard_map/psum | solution.py:75
  334.8 15.7 %multiply_reduce_fusion.2 = (f32[4]{0:T(128)S(1)}, f32[4]{0:T(128)S(1)}, f32[4]{0:T(128)S(1)}, f32[4]{0:T(128)S(1)}, f32[4,4,20,2560]{3,2,1,0:T(8,128)S(1)}) fusion(f32[4,4,26,2560]{3,2,1,0:T(8,128)} %copy-done.5, f32[4,4,20,2560]{3,1,2,0:T(4,128)S(1)} %copy-done.1, f32[4,4,24,2560]{3,2,1,0:T(8,128)} %copy-done.3, f32[4,4,22,2560]{3,2,1,0:T(8,128)} %copy-done.4, ...), kind=kOutput, calls=%fused_computation.53 | convolution fusion | flops 313625600 | bytes 26263308 | tf_op jit(solution)/shard_map/dot_general | solution.py:85
  350.5 3.8 copy.19
  354.3 29.5 %all-reduce.4 = (f32[1,4]{1,0:T(1,128)S(1)}, f32[1,4]{1,0:T(1,128)S(1)}, f32[1,4]{1,0:T(1,128)S(1)}, f32[1,4]{1,0:T(1,128)S(1)}) all-reduce(f32[1,4]{1,0:T(1,128)S(1)} %bitcast.80, f32[1,4]{1,0:T(1,128)S(1)} %bitcast.79, f32[1,4]{1,0:T(1,128)S(1)} %bitcast.78, f32[1,4]{1,0:T(1,128)S(1)} %bitcast.77), channel_id=1, replica_groups=mesh['ens'=2,'gx'=16] {'gx'}, use_global_device_ids=true, to_apply=%region_11.12 | all-reduce | flops 16 | bytes 128 | tf_op jit(solution)/shard_map/psum | solution.py:99
  (44 shorter events, 13.3 us)
Async XLA Ops:
  0.6 12.5 %copy-start = (f32[8,4]{0,1:T(4,128)S(1)}, f32[8,4]{0,1:T(4,128)}, u32[]{:S(2)}) copy-start(f32[8,4]{0,1:T(4,128)} %param.11) | copy-start | bytes 388
  0.6 12.4 %copy-start.8 = (s32[4]{0:T(128)S(1)}, s32[4]{0:T(128)}, u32[]{:S(2)}) copy-start(s32[4]{0:T(128)} %param.10) | copy-start | bytes 52
  0.7 12.7 %copy-start.1 = (f32[4,4,20,2560]{3,1,2,0:T(4,128)S(1)}, f32[4,4,20,2560]{3,1,2,0:T(4,128)}, u32[]{:S(2)}) copy-start(f32[4,4,20,2560]{3,1,2,0:T(4,128)} %param.7) | copy-start | bytes 9830404
  3.8 1.9 copy-start.2
  6.9 84.9 %collective-permute-start = (f32[4,4,4,2560]{3,2,1,0:T(4,128)}, f32[4,4,4,2560]{3,2,1,0:T(4,128)}, u32[]{:S(2)}, u32[]{:S(2)}) collective-permute-start(f32[4,4,4,2560]{3,2,1,0:T(4,128)} %get-tuple-element.12), channel_id=1, source_target_pairs={{0,1},{1,2},{2,3},{3,4},{4,5},{5,6},{6,7},{7,8},{8,9},{9,10},{10,1... | collective-permute-start | bytes 1966088 | tf_op jit(solution)/shard_map/ppermute | solution.py:20
  10.2 81.7 %collective-permute-start.1 = (f32[4,4,4,2560]{3,2,1,0:T(4,128)}, f32[4,4,4,2560]{3,2,1,0:T(4,128)}, u32[]{:S(2)}, u32[]{:S(2)}) collective-permute-start(f32[4,4,4,2560]{3,2,1,0:T(4,128)} %get-tuple-element.13), channel_id=1, source_target_pairs={{1,0},{2,1},{3,2},{4,3},{5,4},{6,5},{7,6},{8,7},{9,8},{10,9},{11,1... | collective-permute-start | bytes 1966088 | tf_op jit(solution)/shard_map/ppermute | solution.py:22
  13.4 3.6 copy-start.7
  17.0 4.7 %copy-start.6 = (s32[30]{0:T(128)S(1)}, s32[30]{0:T(128)}, u32[]{:S(2)}) copy-start(s32[30]{0:T(128)} %param.8) | copy-start | bytes 364
  102.9 5.5 %copy-start.5 = (f32[4,4,26,2560]{3,2,1,0:T(8,128)}, f32[4,4,26,2560]{3,2,1,0:T(8,128)S(1)}, u32[]{:S(2)}) copy-start(f32[4,4,26,2560]{3,2,1,0:T(8,128)S(1)} %fusion.5) | copy-start | bytes 12779524
  183.9 5.2 %copy-start.3 = (f32[4,4,24,2560]{3,2,1,0:T(8,128)}, f32[4,4,24,2560]{3,2,1,0:T(8,128)S(1)}, u32[]{:S(2)}) copy-start(f32[4,4,24,2560]{3,2,1,0:T(8,128)S(1)} %fusion.12) | copy-start | bytes 11796484
  264.7 5.2 %copy-start.4 = (f32[4,4,22,2560]{3,2,1,0:T(8,128)}, f32[4,4,22,2560]{3,2,1,0:T(8,128)S(1)}, u32[]{:S(2)}) copy-start(f32[4,4,22,2560]{3,2,1,0:T(8,128)S(1)} %fusion.13) | copy-start | bytes 10813444
where the time goes:
time: 392 us; the launch traced here: 385 us
  blocking collectives  278 us (71%)
  matrix products  68.8 us (18%)
  local copies, waits for them, and re-layouts  21.9 us (6%)
  other arithmetic  10.1 us (3%)
  starting transfers between devices  4.53 us (1%)
    psum x4, blocking collectives, local(): coeffs = lax.psum(mode_partial_value, 'gx')  249 us
    dot_general x4, matrix products, local(): jnp.dot(partial_value.reshape(-1, partial_value.shape[-1]), table_north,...  42.6 us
    psum x1, blocking collectives, local(): records.append(lax.psum(squares, 'gx'))  29.5 us
    dot_general x4, matrix products, local(): jnp.dot((driving - current).reshape(-1, north_cells), table_north.T, prec...  20.6 us
    unnamed x24, local copies, waits for them, and re-layouts  12.3 us
    slice x4, local copies, waits for them, and re-layouts, local(): extended[:, :, 1:-1]  8.25 us
  transfers between devices with their start and end apart: 2, of which 0 were waited for; matrix products, arithmetic and copies ran while one was open for 3% of the time, Pallas kernels for 0%

commit v1 on v0

v1 whole, which is shorter than its diff:
```python
import functools
import math

import jax
import jax.numpy as jnp
from jax import lax
from jax.experimental import pallas as pl
from jax.experimental.pallas import tpu as pltpu
from jax.sharding import PartitionSpec as P

ITERS = 4
DIFFUSION = 0.24
LANES = 128
MESH = pl.DeviceIdType.MESH
F32 = jnp.float32
BF16 = jnp.bfloat16


def split2(value):
    high = value.astype(BF16)
    return high, (value - high.astype(F32)).astype(BF16)


def sine_of(product, half_period):
    turns = jnp.floor(product * (0.5 / half_period))
    rest = product - turns * (2.0 * half_period) - half_period
    size = jnp.abs(rest)
    fold = jnp.minimum(size, half_period - size) * (math.pi / half_period)
    x = jnp.where(rest > 0, -fold, fold)
    y = x * x
    tail = -1.0 / 6 + y * (1.0 / 120 + y * (-1.0 / 5040 + y * (1.0 / 362880 - y / 39916800)))
    return x + x * (y * tail)


def kernel(
    n, norm, state, drive, modes_e, modes_n, classes, table, out, stat,
    buf_a, buf_b, drv, nproj, csend, crecv, qbuf, sacc, sbuf, tab, east,
    load_sem, out_sem, halo_send, halo_recv, ex_send, ex_recv,
):
    fields, cols, levels, ny = state.shape
    nf = fields * levels
    kx, ky = modes_e.shape[0], modes_n.shape[0]
    nx = cols * n
    pairs = east.shape[0]
    rows_each = csend.shape[1]
    per = nf // rows_each
    h = ITERS
    ext = cols + 2 * h
    me = lax.axis_index("gx")
    has_left, has_right = me > 0, me < n - 1
    inner = pl.ds(LANES, ny)

    barrier = pltpu.get_barrier_semaphore()

    def greet(d, carry):
        pl.semaphore_signal(
            barrier, inc=1, device_id={"gx": lax.rem(me + d, n)}, device_id_type=MESH
        )
        return carry

    lax.fori_loop(1, n, greet, 0)

    for f in range(fields):
        of_f = pl.ds(f * levels, levels)
        pltpu.make_async_copy(
            state.at[f], buf_a.at[pl.ds(h, cols), of_f, inner], load_sem.at[0]
        ).start()
    for f in range(fields):
        of_f = pl.ds(f * levels, levels)
        pltpu.make_async_copy(drive.at[f], drv.at[:, of_f], load_sem.at[1]).start()

    guard = jnp.zeros((ext, nf, LANES), F32)
    for buf in (buf_a, buf_b):
        buf[:, :, 0:LANES] = guard
        buf[:, :, ny + LANES : ny + 2 * LANES] = guard

    line = lax.broadcasted_iota(jnp.int32, (32, LANES), 0)
    wave = jnp.zeros((32, LANES), F32)
    for b in range(ky):
        wave = jnp.where(line == b, modes_n[b].astype(F32), wave)
    place = lax.broadcasted_iota(jnp.int32, (32, LANES), 1).astype(F32) + 1.0

    def north_block(k, carry):
        at = pl.ds(pl.multiple_of(k * LANES, LANES), LANES)
        first = (k * LANES).astype(F32)
        high, low = split2(sine_of(wave * (place + first), ny + 1))
        tab[:, at] = jnp.concatenate([high, high, low, low], axis=0)
        return carry

    lax.fori_loop(0, ny // LANES, north_block, 0)

    spot = (lax.broadcasted_iota(jnp.int32, (cols, LANES), 0) + (me * cols + 1)).astype(F32)
    half = lax.broadcasted_iota(jnp.int32, (cols, LANES), 1) // 64
    for p in range(pairs):
        waves = [modes_e[a].astype(F32) if a < kx else 0.0 for a in (2 * p, 2 * p + 1)]
        east[p] = sine_of(jnp.where(half == 0, waves[0], waves[1]) * spot, nx + 1)

    own = buf_a.at[pl.ds(h, cols), :, inner]
    pltpu.make_async_copy(own, own, load_sem.at[0]).wait()
    pl.semaphore_wait(barrier, n - 1)

    def halo(src_row, dst_row, target, side):
        return pltpu.make_async_remote_copy(
            src_ref=buf_a.at[pl.ds(src_row, h), :, inner],
            dst_ref=buf_a.at[pl.ds(dst_row, h), :, inner],
            send_sem=halo_send.at[side],
            recv_sem=halo_recv.at[side],
            device_id={"gx": target},
            device_id_type=MESH,
        )

    to_right = halo(cols, 0, lax.rem(me + 1, n), 0)
    to_left = halo(h, h + cols, lax.rem(me + n - 1, n), 1)

    @pl.when(has_right)
    def _():
        to_right.start()

    @pl.when(has_left)
    def _():
        to_left.start()

    @pl.when(jnp.logical_not(has_left))
    def _():
        buf_a[h - 1, :, inner] = jnp.zeros((nf, ny), F32)
        for k in range(1, h):
            buf_a[h - 1 - k, :, inner] = -buf_a[h - 1 + k, :, inner]

    @pl.when(jnp.logical_not(has_right))
    def _():
        edge = h + cols
        buf_a[edge, :, inner] = jnp.zeros((nf, ny), F32)
        for k in range(1, h):
            buf_a[edge + k, :, inner] = -buf_a[edge - k, :, inner]

    kc = 512 if ny % 512 == 0 else LANES

    def project(load):
        total = jnp.zeros((2 * cols * nf, LANES), F32)
        for c in range(ny // kc):
            high, low = split2(load(c * kc).reshape(cols * nf, kc))
            total += lax.dot_general(
                jnp.concatenate([high, low], axis=0),
                tab[:, c * kc : (c + 1) * kc],
                (((1,), (1,)), ((), ())),
                preferred_element_type=F32,
            )
        both = total[: cols * nf] + total[cols * nf :]
        return both + pltpu.roll(both, 64, 1)

    proj_u = project(lambda k: buf_a[h : h + cols, :, LANES + k : LANES + k + kc])
    pltpu.make_async_copy(drv, drv, load_sem.at[1]).wait()
    proj_d = project(lambda k: drv[:, :, k : k + kc])
    group = lax.broadcasted_iota(jnp.int32, (cols * nf, LANES), 1) // 32 % 2
    nproj[...] = jnp.where(group == 0, proj_d, proj_u).reshape(cols, nf, LANES)

    def east_project(p, carry):
        acc = jnp.zeros((nf, LANES), F32)
        for x in range(cols):
            acc += east[p, x : x + 1, :] * nproj[x]
        for k in range(per):
            csend[p * per + k] = acc[k * rows_each : (k + 1) * rows_each]
        return carry

    lax.fori_loop(0, pairs, east_project, 0)

    def exchange(source, target_slot, idx):
        def one(d, carry):
            t = lax.rem(me + d, n)
            pltpu.make_async_remote_copy(
                src_ref=source(t),
                dst_ref=target_slot(d),
                send_sem=ex_send.at[idx],
                recv_sem=ex_recv.at[idx],
                device_id={"gx": t},
                device_id_type=MESH,
            ).start()
            return carry

        lax.fori_loop(1, n, one, 0)

    def all_of(buf, sem):
        part = buf.at[pl.ds(0, n - 1)]
        pltpu.make_async_copy(part, part, sem).wait()

    exchange(lambda t: csend.at[t], lambda d: crecv.at[d - 1], 0)

    width = ny // 2 if ny % 256 == 0 else ny

    def diffuse(src, dst, reach, index):
        def row(x, acc, counted):
            for c in range(ny // width):
                lo = c * width
                window = src[x, :, lo : lo + width + 2 * LANES]
                left = pltpu.roll(window, 1, 1)[:, LANES:-LANES]
                right = pltpu.roll(window, width + 2 * LANES - 1, 1)[:, LANES:-LANES]
                mid = slice(lo + LANES, lo + LANES + width)
                sides = (left + right) + (src[x - 1, :, mid] + src[x + 1, :, mid])
                new = (1.0 - 4.0 * DIFFUSION) * window[:, LANES:-LANES] + DIFFUSION * sides
                dst[x, :, mid] = new
                if counted:
                    gap = drv[x - h, :, lo : lo + width] - new
                    gap = gap * gap
                    for t in range(width // LANES):
                        acc += gap[:, t * LANES : (t + 1) * LANES]
            return acc

        zero = jnp.zeros((nf, LANES), F32)
        if reach > 0:
            lax.fori_loop(h - reach, h, lambda x, a: row(x, a, False), zero)
            lax.fori_loop(h + cols, h + cols + reach, lambda x, a: row(x, a, False), zero)
        sacc[index] = lax.fori_loop(h, h + cols, lambda x, a: row(x, a, True), zero)

    @pl.when(has_left)
    def _():
        to_right.wait_recv()

    @pl.when(has_right)
    def _():
        to_left.wait_recv()

    diffuse(buf_a, buf_b, 3, 0)

    @pl.when(has_right)
    def _():
        to_right.wait_send()

    @pl.when(has_left)
    def _():
        to_left.wait_send()

    diffuse(buf_b, buf_a, 2, 1)

    all_of(crecv, ex_recv.at[0])
    mine = lax.fori_loop(0, n - 1, lambda k, a: a + crecv[k], csend[me]) * norm
    lane = lax.broadcasted_iota(jnp.int32, (rows_each, LANES), 1)
    target = jnp.where(lane // 32 % 2 == 0, mine, 0.0)
    start = jnp.where(lane // 32 % 2 == 0, pltpu.roll(mine, LANES - 32, 1), 0.0)
    pair = me // per
    entry = lax.broadcasted_iota(jnp.int32, (rows_each, LANES), 0) + me % per * rows_each
    first, second = (modes_e[jnp.minimum(2 * pair + k, kx - 1)].astype(F32) for k in (0, 1))
    wave_e = jnp.where(lane < 64, first, second)
    wave_n = jnp.zeros((rows_each, LANES), F32)
    for b in range(ky):
        wave_n = jnp.where(lane % 32 == b, modes_n[b].astype(F32), wave_n)
    damp = sine_of(wave_e, 2 * (nx + 1)) ** 2 + sine_of(wave_n, 2 * (ny + 1)) ** 2
    mu = 1.0 - 4.0 * DIFFUSION * damp
    w = jnp.zeros((rows_each, LANES), F32)
    for f in range(fields):
        for l in range(levels):
            w = jnp.where(entry == f * levels + l, table[f, classes[l]], w)
    valid = (2 * pair + lane // 64 < kx) & (lane % 64 < ky)
    w = jnp.where(valid, w, 0.0)
    q = jnp.zeros_like(target)
    free = start
    fixes = []
    for s in range(ITERS):
        q = mu * q + w * (target - (free + q))
        free = mu * free
        fixes.append(q * (q - 2.0 * (target - free)) * (1.0 / norm))
    qbuf[me] = q
    exchange(lambda t: qbuf.at[me], lambda d: qbuf.at[me], 1)

    diffuse(buf_a, buf_b, 1, 2)
    diffuse(buf_b, buf_a, 0, 3)

    lane = lax.broadcasted_iota(jnp.int32, (8, LANES), 1)
    line = lax.broadcasted_iota(jnp.int32, (8, LANES), 0)
    owner = lax.broadcasted_iota(jnp.int32, (nf, LANES), 0) // levels
    local = jnp.zeros((8, LANES), F32)
    for s in range(ITERS):
        for f in range(fields):
            both = jnp.sum(jnp.where(owner == f, sacc[s], 0.0), axis=0, keepdims=True)
            both += jnp.sum(
                jnp.where(entry // levels == f, fixes[s], 0.0), axis=0, keepdims=True
            )
            both = jnp.sum(both, axis=1, keepdims=True)
            local = jnp.where((line == s) & (lane == f), both, local)
    sbuf[me] = local
    exchange(lambda t: sbuf.at[me], lambda d: sbuf.at[me], 2)

    all_of(qbuf, ex_recv.at[1])

    def rebuild(x, carry):
        acc = jnp.zeros((nf, LANES), F32)
        for p in range(pairs):
            if per == 1:
                rows = qbuf[p]
            else:
                rows = jnp.concatenate([qbuf[p * per + k] for k in range(per)], axis=0)
            acc += east[p, pl.ds(x, 1), :] * rows
        nproj[x] = acc + pltpu.roll(acc, 64, 1)
        return carry

    lax.fori_loop(0, cols, rebuild, 0)
    step = 4 if cols % 4 == 0 else 1
    lane = lax.broadcasted_iota(jnp.int32, (step * nf, LANES), 1)
    for g in range(cols // step):
        coeff = nproj[g * step : (g + 1) * step].reshape(step * nf, LANES)
        rest = coeff - coeff.astype(BF16).astype(F32)
        lhs = jnp.where(lane // 32 % 2 == 0, coeff, pltpu.roll(rest, 32, 1)).astype(BF16)
        for c in range(ny // kc):
            sl = slice(c * kc, (c + 1) * kc)
            part = jnp.dot(lhs, tab[:, sl], preferred_element_type=F32)
            drv[g * step : (g + 1) * step, :, sl] = (
                part.reshape(step, nf, kc)
                + buf_a[h + g * step : h + (g + 1) * step, :, LANES + c * kc : LANES + (c + 1) * kc]
            )
        some = pl.ds(g * step, step)
        for f in range(fields):
            pltpu.make_async_copy(
                drv.at[some, pl.ds(f * levels, levels)], out.at[f, some], out_sem
            ).start()

    all_of(sbuf, ex_recv.at[2])
    squares = lax.fori_loop(1, n, lambda k, a: a + sbuf[k], sbuf[0])
    cells = float(levels * nx * ny)
    stat[...] = jnp.sqrt(jnp.maximum(squares[:ITERS, :fields], 0.0) / cells)
    all_of(crecv, ex_send.at[0])
    all_of(qbuf, ex_send.at[1])
    all_of(sbuf, ex_send.at[2])
    pltpu.make_async_copy(drv, drv, out_sem).wait()


def local(model_state, driving, mode_east, mode_north, level_class, nudge_table):
    fields, levels, cols, ny = model_state.shape
    nf = fields * levels
    n = lax.axis_size("gx")
    nx = cols * n
    norm = 4.0 / ((nx + 1) * (ny + 1))
    pairs = 16
    rows_each = pairs * nf // n
    ext = cols + 2 * ITERS
    any_space = pl.BlockSpec(memory_space=pl.ANY)
    vmem = pl.BlockSpec(memory_space=pltpu.VMEM)
    smem = pl.BlockSpec(memory_space=pltpu.SMEM)
    out, stat = pl.pallas_call(
        functools.partial(kernel, n, norm),
        out_shape=(
            jax.ShapeDtypeStruct((fields, cols, levels, ny), F32),
            jax.ShapeDtypeStruct((ITERS, fields), F32),
        ),
        in_specs=[any_space, any_space, smem, smem, smem, smem],
        out_specs=(any_space, vmem),
        scratch_shapes=[
            pltpu.VMEM((ext, nf, ny + 2 * LANES), F32),
            pltpu.VMEM((ext, nf, ny + 2 * LANES), F32),
            pltpu.VMEM((cols, nf, ny), F32),
            pltpu.VMEM((cols, nf, LANES), F32),
            pltpu.VMEM((n, rows_each, LANES), F32),
            pltpu.VMEM((n, rows_each, LANES), F32),
            pltpu.VMEM((n, rows_each, LANES), F32),
            pltpu.VMEM((ITERS, nf, LANES), F32),
            pltpu.VMEM((n, 8, LANES), F32),
            pltpu.VMEM((LANES, ny), BF16),
            pltpu.VMEM((pairs, cols, LANES), F32),
            pltpu.SemaphoreType.DMA((2,)),
            pltpu.SemaphoreType.DMA,
            pltpu.SemaphoreType.DMA((2,)),
            pltpu.SemaphoreType.DMA((2,)),
            pltpu.SemaphoreType.DMA((3,)),
            pltpu.SemaphoreType.DMA((3,)),
        ],
        compiler_params=pltpu.CompilerParams(collective_id=0, has_side_effects=True),
    )(
        model_state.transpose(0, 2, 1, 3),
        driving.transpose(0, 2, 1, 3),
        mode_east, mode_north, level_class, nudge_table.T,
    )
    return out.transpose(0, 2, 1, 3), stat


def solution(mesh):
    return jax.shard_map(
        local,
        mesh=mesh,
        in_specs=(P("ens", None, "gx", None), P("ens", None, "gx", None), P(), P(), P(), P()),
        out_specs=(P("ens", None, "gx", None), P("ens", None)),
        check_vma=False,
    )
```

time: 392 us -> 49 us (0.12); the launches traced: 385 us -> 48.9 us
  blocking collectives: 278 us -> 0 us
  matrix products: 68.8 us -> 0 us
  Pallas kernels: 0 us -> 43.7 us
  local copies, waits for them, and re-layouts: 21.9 us -> 4.55 us
  other arithmetic: 10.1 us -> 0 us
  starting transfers between devices: 4.53 us -> 0 us
    psum x5 -> x0, blocking collectives: 278 us -> none  [the longest x4 249 us: local(): coeffs = lax.psum(mode_partial_value, 'gx')]
    dot_general x17 -> x0, matrix products: 68.8 us -> none  [the longest x4 42.6 us: local(): jnp.dot(partial_value.reshape(-1, partial_value.shape[-1]), table_north,...]
    pallas_call x0 -> x1, Pallas kernels: none -> 43.7 us  [local(): pl.pallas_call(functools.partial(kernel, n, norm), out_shape=(jax.ShapeDt...]
    slice x5 -> x0, local copies, waits for them, and re-layouts: 9.5 us -> none  [the longest x4 8.25 us: local(): extended[:, :, 1:-1]]
    unnamed x24 -> x4, local copies, waits for them, and re-layouts: 12.3 us -> 4.55 us
    ppermute x2 -> x0, starting transfers between devices: 4.53 us -> none  [the longest x1 3.25 us: extended_2(): lax.ppermute(tail, axis, [(i, (i + 1) % count) for i in range(ends)])]
  transfers between devices with their start and end apart: 2 -> 0, of which waited for: 0 -> 0; matrix products, arithmetic and copies ran while one was open for 3% -> 0% of each run, Pallas kernels for 0% -> 0%
where the time goes in v1:
time: 49 us; the launch traced here: 48.9 us
  Pallas kernels  43.7 us (89%)
  local copies, waits for them, and re-layouts  4.55 us (9%)
  between operations  0.65 us (1%)
    pallas_call x1, Pallas kernels, local(): pl.pallas_call(functools.partial(kernel, n, norm), out_shape=(jax.ShapeDt...  43.7 us
    unnamed x4, local copies, waits for them, and re-layouts  4.55 us

profile of v1, /device:TPU:0, one launch (start us, length us, event | category | flops | bytes accessed | tf_op | source)
XLA Modules:
  0.0 48.9 jit_solution(18203483638174115270)
XLA Ops:
  0.6 43.7 %shard_map.77 = (f32[4,20,4,2560]{3,2,1,0:T(4,128)}, f32[4,4]{1,0:T(4,128)}) custom-call(f32[4,20,4,2560]{3,2,1,0:T(4,128)} %bitcast.5, f32[4,20,4,2560]{3,2,1,0:T(4,128)} %bitcast.6, s32[30]{0:T(128)} %modes_e.1, s32[30]{0:T(128)} %modes_n.1, s32[4]{0:T(128)} %classes.1, f32[4,8]{1,0:T(4,128)} %bitcast.7), custom_call_target="tpu_custom_call" | custom-call | tf_op jit(solution)/shard_map/pallas_call | solution.py:337
  44.3 0.0 copy-start
  44.3 4.0 %copy.10 = f32[4,4,20,2560]{3,1,2,0:T(4,128)} copy(f32[4,4,20,2560]{3,1,2,0:T(4,128)} %bitcast.4) | data formatting | bytes 6553600
  48.3 0.0 copy-done
  48.3 0.6 %copy.11 = f32[4,4]{1,0:T(4,128)} copy(f32[4,4]{1,0:T(4,128)S(1)} %copy-done) | data formatting | bytes 128
Async XLA Ops:
  44.3 4.0 %copy-start = (f32[4,4]{1,0:T(4,128)S(1)}, f32[4,4]{1,0:T(4,128)}, u32[]{:S(2)}) copy-start(f32[4,4]{1,0:T(4,128)} %get-tuple-element.9) | copy-start | bytes 196

commit v2 on v1

--- a/solution.py
+++ b/solution.py
@@ -33,8 +33,8 @@
 
 
 def kernel(
-    n, norm, state, drive, modes_e, modes_n, classes, table, out, stat,
-    buf_a, buf_b, drv, nproj, csend, crecv, qbuf, sacc, sbuf, tab, east,
+    n, norm, state, drive, modes_e, modes_n, classes, table, free_out, nproj, tab, stat,
+    buf_a, buf_b, drv, csend, crecv, qbuf, sacc, sbuf, east,
     load_sem, out_sem, halo_send, halo_recv, ex_send, ex_recv,
 ):
     fields, cols, levels, ny = state.shape
@@ -74,6 +74,31 @@
         buf[:, :, 0:LANES] = guard
         buf[:, :, ny + LANES : ny + 2 * LANES] = guard
 
+    pl.semaphore_wait(barrier, n - 1)
+
+    def halo(src_row, dst_row, target, side):
+        for f in range(fields):
+            pltpu.make_async_remote_copy(
+                src_ref=state.at[f, pl.ds(src_row, h)],
+                dst_ref=buf_a.at[pl.ds(dst_row, h), pl.ds(f * levels, levels), inner],
+                send_sem=halo_send.at[side],
+                recv_sem=halo_recv.at[side],
+                device_id={"gx": target},
+                device_id_type=MESH,
+            ).start()
+
+    @pl.when(has_right)
+    def _():
+        halo(cols - h, 0, lax.rem(me + 1, n), 0)
+
+    @pl.when(has_left)
+    def _():
+        halo(0, h + cols, lax.rem(me + n - 1, n), 1)
+
+    def halo_done(row, sem):
+        part = buf_a.at[pl.ds(row, h), :, inner]
+        pltpu.make_async_copy(part, part, sem).wait()
+
     line = lax.broadcasted_iota(jnp.int32, (32, LANES), 0)
     wave = jnp.zeros((32, LANES), F32)
     for b in range(ky):
@@ -97,28 +122,6 @@
 
     own = buf_a.at[pl.ds(h, cols), :, inner]
     pltpu.make_async_copy(own, own, load_sem.at[0]).wait()
-    pl.semaphore_wait(barrier, n - 1)
-
-    def halo(src_row, dst_row, target, side):
-        return pltpu.make_async_remote_copy(
-            src_ref=buf_a.at[pl.ds(src_row, h), :, inner],
-            dst_ref=buf_a.at[pl.ds(dst_row, h), :, inner],
-            send_sem=halo_send.at[side],
-            recv_sem=halo_recv.at[side],
-            device_id={"gx": target},
-            device_id_type=MESH,
-        )
-
-    to_right = halo(cols, 0, lax.rem(me + 1, n), 0)
-    to_left = halo(h, h + cols, lax.rem(me + n - 1, n), 1)
-
-    @pl.when(has_right)
-    def _():
-        to_right.start()
-
-    @pl.when(has_left)
-    def _():
-        to_left.start()
 
     @pl.when(jnp.logical_not(has_left))
     def _():
@@ -187,7 +190,7 @@
 
     width = ny // 2 if ny % 256 == 0 else ny
 
-    def diffuse(src, dst, reach, index):
+    def diffuse(src, dst, plain, counted_rows):
         def row(x, acc, counted):
             for c in range(ny // width):
                 lo = c * width
@@ -206,30 +209,24 @@
             return acc
 
         zero = jnp.zeros((nf, LANES), F32)
-        if reach > 0:
-            lax.fori_loop(h - reach, h, lambda x, a: row(x, a, False), zero)
-            lax.fori_loop(h + cols, h + cols + reach, lambda x, a: row(x, a, False), zero)
-        sacc[index] = lax.fori_loop(h, h + cols, lambda x, a: row(x, a, True), zero)
-
-    @pl.when(has_left)
-    def _():
-        to_right.wait_recv()
-
-    @pl.when(has_right)
-    def _():
-        to_left.wait_recv()
-
-    diffuse(buf_a, buf_b, 3, 0)
-
-    @pl.when(has_right)
-    def _():
-        to_right.wait_send()
-
-    @pl.when(has_left)
-    def _():
-        to_left.wait_send()
-
-    diffuse(buf_b, buf_a, 2, 1)
+        for lo, hi in plain:
+            if hi > lo:
+                lax.fori_loop(lo, hi, lambda x, a: row(x, a, False), zero)
+        total = zero
+        for lo, hi in counted_rows:
+            total = lax.fori_loop(lo, hi, lambda x, a: row(x, a, True), total)
+        return total
+
+    end = h + cols
+    for s in range(1, ITERS + 1):
+        src, dst = (buf_a, buf_b) if s % 2 else (buf_b, buf_a)
+        sacc[s - 1] = diffuse(src, dst, [], [(h + s, end - s)])
+    inside = pltpu.make_async_copy(
+        buf_a.at[pl.ds(2 * h, cols - 2 * h), :, inner],
+        free_out.at[pl.ds(h, cols - 2 * h)],
+        out_sem,
+    )
+    inside.start()
 
     all_of(crecv, ex_recv.at[0])
     mine = lax.fori_loop(0, n - 1, lambda k, a: a + crecv[k], csend[me]) * norm
@@ -261,8 +258,27 @@
     qbuf[me] = q
     exchange(lambda t: qbuf.at[me], lambda d: qbuf.at[me], 1)
 
-    diffuse(buf_a, buf_b, 1, 2)
-    diffuse(buf_b, buf_a, 0, 3)
+    @pl.when(has_left)
+    def _():
+        halo_done(0, halo_recv.at[0])
+
+    @pl.when(has_right)
+    def _():
+        halo_done(end, halo_recv.at[1])
+
+    for s in range(1, ITERS + 1):
+        src, dst = (buf_a, buf_b) if s % 2 else (buf_b, buf_a)
+        sacc[s - 1] += diffuse(
+            src, dst, [(s, h), (end, end + h - s)], [(h, h + s), (end - s, end)]
+        )
+    west, east_edge = (
+        pltpu.make_async_copy(
+            buf_a.at[pl.ds(first, h), :, inner], free_out.at[pl.ds(first - h, h)], out_sem
+        )
+        for first in (h, end - h)
+    )
+    west.start()
+    east_edge.start()
 
     lane = lax.broadcasted_iota(jnp.int32, (8, LANES), 1)
     line = lax.broadcasted_iota(jnp.int32, (8, LANES), 0)
@@ -293,33 +309,55 @@
         return carry
 
     lax.fori_loop(0, cols, rebuild, 0)
+    all_of(sbuf, ex_recv.at[2])
+    squares = lax.fori_loop(1, n, lambda k, a: a + sbuf[k], sbuf[0])
+    stat[...] = squares
+    all_of(crecv, ex_send.at[0])
+    all_of(qbuf, ex_send.at[1])
+    all_of(sbuf, ex_send.at[2])
+
+    @pl.when(has_right)
+    def _():
+        halo_done(0, halo_send.at[0])
+
+    @pl.when(has_left)
+    def _():
+        halo_done(end, halo_send.at[1])
+
+    pltpu.make_async_copy(drv, drv, out_sem).wait()
+
+
+def finish(cells, free, coeffs, tab, squares, out, log, held, load_sem, out_sem):
+    fields, cols, levels, ny = out.shape
+    nf = fields * levels
+    kc = 512 if ny % 512 == 0 else LANES
     step = 4 if cols % 4 == 0 else 1
+    groups = cols // step
+    loads = [
+        pltpu.make_async_copy(
+            free.at[pl.ds(g * step, step)], held.at[pl.ds(g * step, step)], load_sem.at[g]
+        )
+        for g in range(groups)
+    ]
+    for load in loads:
+        load.start()
+    log[...] = jnp.sqrt(jnp.maximum(squares[:ITERS, :fields], 0.0) / cells)
     lane = lax.broadcasted_iota(jnp.int32, (step * nf, LANES), 1)
-    for g in range(cols // step):
-        coeff = nproj[g * step : (g + 1) * step].reshape(step * nf, LANES)
+    for g in range(groups):
+        coeff = coeffs[g * step : (g + 1) * step].reshape(step * nf, LANES)
         rest = coeff - coeff.astype(BF16).astype(F32)
         lhs = jnp.where(lane // 32 % 2 == 0, coeff, pltpu.roll(rest, 32, 1)).astype(BF16)
+        loads[g].wait()
         for c in range(ny // kc):
             sl = slice(c * kc, (c + 1) * kc)
             part = jnp.dot(lhs, tab[:, sl], preferred_element_type=F32)
-            drv[g * step : (g + 1) * step, :, sl] = (
-                part.reshape(step, nf, kc)
-                + buf_a[h + g * step : h + (g + 1) * step, :, LANES + c * kc : LANES + (c + 1) * kc]
-            )
+            held[g * step : (g + 1) * step, :, sl] += part.reshape(step, nf, kc)
         some = pl.ds(g * step, step)
         for f in range(fields):
             pltpu.make_async_copy(
-                drv.at[some, pl.ds(f * levels, levels)], out.at[f, some], out_sem
+                held.at[some, pl.ds(f * levels, levels)], out.at[f, some], out_sem
             ).start()
-
-    all_of(sbuf, ex_recv.at[2])
-    squares = lax.fori_loop(1, n, lambda k, a: a + sbuf[k], sbuf[0])
-    cells = float(levels * nx * ny)
-    stat[...] = jnp.sqrt(jnp.maximum(squares[:ITERS, :fields], 0.0) / cells)
-    all_of(crecv, ex_send.at[0])
-    all_of(qbuf, ex_send.at[1])
-    all_of(sbuf, ex_send.at[2])
-    pltpu.make_async_copy(drv, drv, out_sem).wait()
+    pltpu.make_async_copy(held, held, out_sem).wait()
 
 
 def local(model_state, driving, mode_east, mode_north, level_class, nudge_table):
@@ -334,25 +372,25 @@
     any_space = pl.BlockSpec(memory_space=pl.ANY)
     vmem = pl.BlockSpec(memory_space=pltpu.VMEM)
     smem = pl.BlockSpec(memory_space=pltpu.SMEM)
-    out, stat = pl.pallas_call(
+    free, coeffs, tab, squares = pl.pallas_call(
         functools.partial(kernel, n, norm),
         out_shape=(
-            jax.ShapeDtypeStruct((fields, cols, levels, ny), F32),
-            jax.ShapeDtypeStruct((ITERS, fields), F32),
+            jax.ShapeDtypeStruct((cols, nf, ny), F32),
+            jax.ShapeDtypeStruct((cols, nf, LANES), F32),
+            jax.ShapeDtypeStruct((LANES, ny), BF16),
+            jax.ShapeDtypeStruct((8, LANES), F32),
         ),
         in_specs=[any_space, any_space, smem, smem, smem, smem],
-        out_specs=(any_space, vmem),
+        out_specs=(any_space, vmem, vmem, vmem),
         scratch_shapes=[
             pltpu.VMEM((ext, nf, ny + 2 * LANES), F32),
             pltpu.VMEM((ext, nf, ny + 2 * LANES), F32),
             pltpu.VMEM((cols, nf, ny), F32),
-            pltpu.VMEM((cols, nf, LANES), F32),
             pltpu.VMEM((n, rows_each, LANES), F32),
             pltpu.VMEM((n, rows_each, LANES), F32),
             pltpu.VMEM((n, rows_each, LANES), F32),
             pltpu.VMEM((ITERS, nf, LANES), F32),
             pltpu.VMEM((n, 8, LANES), F32),
-            pltpu.VMEM((LANES, ny), BF16),
             pltpu.VMEM((pairs, cols, LANES), F32),
             pltpu.SemaphoreType.DMA((2,)),
             pltpu.SemaphoreType.DMA,
@@ -361,13 +399,31 @@
             pltpu.SemaphoreType.DMA((3,)),
             pltpu.SemaphoreType.DMA((3,)),
         ],
-        compiler_params=pltpu.CompilerParams(collective_id=0, has_side_effects=True),
+        compiler_params=pltpu.CompilerParams(
+            collective_id=0, has_side_effects=True, vmem_limit_bytes=60_000_000
+        ),
     )(
         model_state.transpose(0, 2, 1, 3),
         driving.transpose(0, 2, 1, 3),
         mode_east, mode_north, level_class, nudge_table.T,
     )
-    return out.transpose(0, 2, 1, 3), stat
+    step = 4 if cols % 4 == 0 else 1
+    out, log = pl.pallas_call(
+        functools.partial(finish, float(levels * nx * ny)),
+        out_shape=(
+            jax.ShapeDtypeStruct((fields, cols, levels, ny), F32),
+            jax.ShapeDtypeStruct((ITERS, fields), F32),
+        ),
+        in_specs=[any_space, vmem, vmem, vmem],
+        out_specs=(any_space, vmem),
+        scratch_shapes=[
+            pltpu.VMEM((cols, nf, ny), F32),
+            pltpu.SemaphoreType.DMA((cols // step,)),
+            pltpu.SemaphoreType.DMA,
+        ],
+        compiler_params=pltpu.CompilerParams(vmem_limit_bytes=58_000_000),
+    )(free, coeffs, tab, squares)
+    return out.transpose(0, 2, 1, 3), log
 
 
 def solution(mesh):

time: 49 us -> 40.1 us (0.82)
  local copies, waits for them, and re-layouts: 4.55 us -> 0 us
  Pallas kernels: 43.7 us -> 39.3 us
    pallas_call x1, Pallas kernels: 43.7 us -> 34.1 us  [local(): pl.pallas_call(functools.partial(kernel, n, norm), out_shape=(jax.ShapeDt...]
    pallas_call x0 -> x1, Pallas kernels: none -> 5.21 us  [local(): pl.pallas_call(functools.partial(finish, float(levels * nx * ny)), out_sh...]
    unnamed x4 -> x0, local copies, waits for them, and re-layouts: 4.55 us -> none
where the time goes in v2:
time: 40.1 us; the launch traced here: 39.9 us
  Pallas kernels  39.3 us (98%)
  between operations  0.64 us (2%)
    pallas_call x1, Pallas kernels, local(): pl.pallas_call(functools.partial(kernel, n, norm), out_shape=(jax.ShapeDt...  34.1 us
    pallas_call x1, Pallas kernels, local(): pl.pallas_call(functools.partial(finish, float(levels * nx * ny)), out_sh...  5.21 us

profile of v2, /device:TPU:0, one launch (start us, length us, event | category | flops | bytes accessed | tf_op | source)
XLA Modules:
  0.0 39.9 jit_solution(2832017123781942092)
XLA Ops:
  0.6 34.1 %shard_map.77 = (f32[20,16,2560]{2,1,0:T(8,128)}, f32[20,16,128]{2,1,0:T(8,128)}, bf16[128,2560]{1,0:T(8,128)(2,1)}, f32[8,128]{1,0:T(8,128)}) custom-call(f32[4,20,4,2560]{3,2,1,0:T(4,128)} %bitcast.4, f32[4,20,4,2560]{3,2,1,0:T(4,128)} %bitcast.5, s32[30]{0:T(128)} %modes_e.1, s32[30]{0:T(128)} %modes_n.1, s32[4]{0:T(128)} %classes.1, f32[4,8]{1,0:T(4,128)} %bitcast.6), custom_call_target="tpu_custom_call" | custom-call | tf_op jit(solution)/shard_map/pallas_call | solution.py:375
  34.7 5.2 %shard_map.78 = (f32[4,20,4,2560]{3,2,1,0:T(4,128)}, f32[4,4]{1,0:T(4,128)}) custom-call(f32[20,16,2560]{2,1,0:T(8,128)} %get-tuple-element.8.free, f32[20,16,128]{2,1,0:T(8,128)} %get-tuple-element.9.coeffs, bf16[128,2560]{1,0:T(8,128)(2,1)} %get-tuple-element.10.tab, f32[8,128]{1,0:T(8,128)} %get-tuple-element.11.squares), custom_call_target="tpu_custom_call" | custom-call | tf_op jit(solution)/shard_map/pallas_call | solution.py:411

commit v3 on v2

--- a/solution.py
+++ b/solution.py
@@ -76,8 +76,8 @@
 
     pl.semaphore_wait(barrier, n - 1)
 
-    def halo(src_row, dst_row, target, side):
-        for f in range(fields):
+    def halo(src_row, dst_row, target, side, some):
+        for f in some:
             pltpu.make_async_remote_copy(
                 src_ref=state.at[f, pl.ds(src_row, h)],
                 dst_ref=buf_a.at[pl.ds(dst_row, h), pl.ds(f * levels, levels), inner],
@@ -87,13 +87,16 @@
                 device_id_type=MESH,
             ).start()
 
-    @pl.when(has_right)
-    def _():
-        halo(cols - h, 0, lax.rem(me + 1, n), 0)
-
-    @pl.when(has_left)
-    def _():
-        halo(0, h + cols, lax.rem(me + n - 1, n), 1)
+    def halos(some):
+        @pl.when(has_right)
+        def _():
+            halo(cols - h, 0, lax.rem(me + 1, n), 0, some)
+
+        @pl.when(has_left)
+        def _():
+            halo(0, h + cols, lax.rem(me + n - 1, n), 1, some)
+
+    halos(range(fields // 2))
 
     def halo_done(row, sem):
         part = buf_a.at[pl.ds(row, h), :, inner]
@@ -187,6 +190,7 @@
         pltpu.make_async_copy(part, part, sem).wait()
 
     exchange(lambda t: csend.at[t], lambda d: crecv.at[d - 1], 0)
+    halos(range(fields // 2, fields))
 
     width = ny // 2 if ny % 256 == 0 else ny
 

time: 40.1 us -> 39.8 us (level)
  no operation moved by 1% of the time
where the time goes in v3:
time: 39.8 us; the launch traced here: 39.6 us
  Pallas kernels  39 us (98%)
  between operations  0.64 us (2%)
    pallas_call x1, Pallas kernels, local(): pl.pallas_call(functools.partial(kernel, n, norm), out_shape=(jax.ShapeDt...  33.8 us
    pallas_call x1, Pallas kernels, local(): pl.pallas_call(functools.partial(finish, float(levels * nx * ny)), out_sh...  5.21 us

profile of v3, /device:TPU:0, one launch (start us, length us, event | category | flops | bytes accessed | tf_op | source)
XLA Modules:
  0.0 39.6 jit_solution(7954894128156750067)
XLA Ops:
  0.6 33.8 %shard_map.77 = (f32[20,16,2560]{2,1,0:T(8,128)}, f32[20,16,128]{2,1,0:T(8,128)}, bf16[128,2560]{1,0:T(8,128)(2,1)}, f32[8,128]{1,0:T(8,128)}) custom-call(f32[4,20,4,2560]{3,2,1,0:T(4,128)} %bitcast.4, f32[4,20,4,2560]{3,2,1,0:T(4,128)} %bitcast.5, s32[30]{0:T(128)} %modes_e.1, s32[30]{0:T(128)} %modes_n.1, s32[4]{0:T(128)} %classes.1, f32[4,8]{1,0:T(4,128)} %bitcast.6), custom_call_target="tpu_custom_call" | custom-call | tf_op jit(solution)/shard_map/pallas_call | solution.py:379
  34.4 5.2 %shard_map.78 = (f32[4,20,4,2560]{3,2,1,0:T(4,128)}, f32[4,4]{1,0:T(4,128)}) custom-call(f32[20,16,2560]{2,1,0:T(8,128)} %get-tuple-element.8.free, f32[20,16,128]{2,1,0:T(8,128)} %get-tuple-element.9.coeffs, bf16[128,2560]{1,0:T(8,128)(2,1)} %get-tuple-element.10.tab, f32[8,128]{1,0:T(8,128)} %get-tuple-element.11.squares), custom_call_target="tpu_custom_call" | custom-call | tf_op jit(solution)/shard_map/pallas_call | solution.py:415
